TPU v7x, 256 devices: a whole 4x4x8 slice. The times are simulated.
256 devices in a mesh: tp: 4 (over x), fsdp: 64 (over z, y, core).
Axes of the slice: x: 4, y: 4, z: 8, core: 2. Of those that a mesh axis runs over, the one named last changes fastest.
Arguments:
- patches: bfloat16 [4096, 49, 3072], P('fsdp')
- labels: int32 [4096], P('fsdp')
- w_stem: float32 [3072, 512], P('fsdp', 'tp')
- b_stem: float32 [512], P(('tp', 'fsdp'))
- ln1_g: float32 [2, 512], P(None, ('tp', 'fsdp'))
- ln1_b: float32 [2, 512], P(None, ('tp', 'fsdp'))
- w_tok1: float32 [2, 49, 256], P(None, None, 'fsdp')
- b_tok1: float32 [2, 256], P(None, 'fsdp')
- w_tok2: float32 [2, 256, 49], P(None, 'fsdp')
- ln2_g: float32 [2, 512], P(None, ('tp', 'fsdp'))
- ln2_b: float32 [2, 512], P(None, ('tp', 'fsdp'))
- w_ch1: float32 [2, 512, 2048], P(None, 'fsdp', 'tp')
- b_ch1: float32 [2, 2048], P(None, ('tp', 'fsdp'))
- w_ch2: float32 [2, 2048, 512], P(None, ('tp', 'fsdp'))
- b_ch2: float32 [2, 512], P(None, ('tp', 'fsdp'))
- lnf_g: float32 [512], P(('tp', 'fsdp'))
- lnf_b: float32 [512], P(('tp', 'fsdp'))
- w_head: float32 [512, 1000], P('fsdp', 'tp')
- b_head: float32 [1000], P('tp')
Outputs:
- output 1: float32 [], replicated
- output 2: float32 [3072, 512], P('fsdp', 'tp')
- output 3: float32 [512], P(('tp', 'fsdp'))
- output 4: float32 [2, 512], P(None, ('tp', 'fsdp'))
- output 5: float32 [2, 512], P(None, ('tp', 'fsdp'))
- output 6: float32 [2, 49, 256], P(None, None, 'fsdp')
- output 7: float32 [2, 256], P(None, 'fsdp')
- output 8: float32 [2, 256, 49], P(None, 'fsdp')
- output 9: float32 [2, 512], P(None, ('tp', 'fsdp'))
- output 10: float32 [2, 512], P(None, ('tp', 'fsdp'))
- output 11: float32 [2, 512, 2048], P(None, 'fsdp', 'tp')
- output 12: float32 [2, 2048], P(None, ('tp', 'fsdp'))
- output 13: float32 [2, 2048, 512], P(None, ('tp', 'fsdp'))
- output 14: float32 [2, 512], P(None, ('tp', 'fsdp'))
- output 15: float32 [512], P(('tp', 'fsdp'))
- output 16: float32 [512], P(('tp', 'fsdp'))
- output 17: float32 [512, 1000], P('fsdp', 'tp')
- output 18: float32 [1000], P('tp')
All inputs are finite; a program needn't handle non-finite values.
Results may differ from a plain program's by a relative error of at most 0.0136364.
Values are sent between devices in bfloat16 or wider.
A program may use at most 768 MiB of HBM per device.

v0:
```python
import jax
import jax.numpy as jnp
from jax import lax
from jax.sharding import PartitionSpec as P

EPS = 1e-6
CHANNEL_AXES = ('tp', 'fsdp')
LAYER_NAMES = ('ln1_g', 'ln1_b', 'w_tok1', 'b_tok1', 'w_tok2', 'ln2_g', 'ln2_b', 'w_ch1', 'b_ch1', 'w_ch2', 'b_ch2')


def product(form, left, right):
    return jnp.einsum(form, left, right, preferred_element_type=jnp.float32)


def gather_weight(weight, axis):
    return lax.all_gather(weight.astype(jnp.bfloat16), 'fsdp', axis=axis, tiled=True)


def gather_vector(values):
    return lax.all_gather(values, 'fsdp', axis=values.ndim - 1, tiled=True)


def sum_to_piece(grad_full, axis):
    return lax.psum_scatter(grad_full, 'fsdp', scatter_dimension=axis, tiled=True)


def lead_sum(values):
    return jnp.sum(values.reshape(-1, values.shape[-1]), axis=0)


def norm_forward(values, gain, shift, width):
    moments = jnp.concatenate([jnp.sum(values, axis=-1, keepdims=True),
                               jnp.sum(values * values, axis=-1, keepdims=True)], axis=-1)
    moments = lax.psum(moments, 'tp') / width
    mean_val = moments[..., :1]
    inv_std = lax.rsqrt(jnp.maximum(moments[..., 1:] - mean_val * mean_val, 0.0) + EPS)
    standard = (values - mean_val) * inv_std
    return standard * gain + shift, standard, inv_std


def norm_backward(grad_out, gain, standard, inv_std, width):
    grad_std = grad_out * gain
    moments = jnp.concatenate([jnp.sum(grad_std, axis=-1, keepdims=True),
                               jnp.sum(grad_std * standard, axis=-1, keepdims=True)], axis=-1)
    moments = lax.psum(moments, 'tp') / width
    return inv_std * (grad_std - moments[..., :1] - standard * moments[..., 1:])


def gelu_grad(pre_act, grad_out):
    return jax.vjp(jax.nn.gelu, pre_act)[1](grad_out)[0]


def weight_specs():
    vec_spec = P(CHANNEL_AXES)
    layer_vec = P(None, CHANNEL_AXES)
    return (P('fsdp', 'tp'), vec_spec, layer_vec, layer_vec, P(None, None, 'fsdp'), P(None, 'fsdp'),
            P(None, 'fsdp', None), layer_vec, layer_vec, P(None, 'fsdp', 'tp'), layer_vec,
            P(None, CHANNEL_AXES, None), layer_vec, vec_spec, vec_spec, P('fsdp', 'tp'), P('tp'))


def solution(mesh):
    fsdp_size = mesh.shape['fsdp']
    tp_size = mesh.shape['tp']

    def step(patches, labels, w_stem, b_stem, ln1_g, ln1_b, w_tok1, b_tok1, w_tok2,
             ln2_g, ln2_b, w_ch1, b_ch1, w_ch2, b_ch2, lnf_g, lnf_b, w_head, b_head):
        local_images = patches.shape[0]
        tokens = patches.shape[1]
        channels = w_stem.shape[1] * tp_size
        total_images = local_images * fsdp_size
        stem_bias = gather_vector(b_stem)
        ln1_gain = gather_vector(ln1_g)
        ln1_shift = gather_vector(ln1_b)
        tok_bias = gather_vector(b_tok1)
        ln2_gain = gather_vector(ln2_g)
        ln2_shift = gather_vector(ln2_b)
        ch_bias1 = gather_vector(b_ch1)
        ch_bias2 = gather_vector(b_ch2)
        lnf_gain = gather_vector(lnf_g)
        lnf_shift = gather_vector(lnf_b)

        resid = product('bsp,pc->bsc', patches, gather_weight(w_stem, 0)) + stem_bias
        saved = []
        for layer in range(w_tok1.shape[0]):
            normed, norm1_std, norm1_inv = norm_forward(resid, ln1_gain[layer], ln1_shift[layer], channels)
            normed = normed.astype(jnp.bfloat16)
            tok_pre = product('bsc,sj->bcj', normed, gather_weight(w_tok1[layer], 1)) + tok_bias[layer]
            tok_act = jax.nn.gelu(tok_pre).astype(jnp.bfloat16)
            resid = resid + product('bcj,js->bsc', tok_act, gather_weight(w_tok2[layer], 0))
            normed2, norm2_std, norm2_inv = norm_forward(resid, ln2_gain[layer], ln2_shift[layer], channels)
            full_in = lax.all_gather(normed2.astype(jnp.bfloat16), 'tp', axis=2, tiled=True)
            ch_pre = product('bsc,cd->bsd', full_in, gather_weight(w_ch1[layer], 0)) + ch_bias1[layer]
            ch_act = jax.nn.gelu(ch_pre).astype(jnp.bfloat16)
            part_sum = product('bsd,dc->bsc', ch_act, gather_weight(w_ch2[layer], 0))
            resid = resid + lax.psum_scatter(part_sum, 'tp', scatter_dimension=2, tiled=True) + ch_bias2[layer]
            saved.append(dict(normed=normed, norm1_std=norm1_std, norm1_inv=norm1_inv, tok_pre=tok_pre,
                              tok_act=tok_act, norm2_std=norm2_std, norm2_inv=norm2_inv,
                              full_in=full_in, ch_pre=ch_pre, ch_act=ch_act))

        pooled = jnp.mean(resid, axis=1)
        head_in, head_std, head_inv = norm_forward(pooled, lnf_gain, lnf_shift, channels)
        head_full = lax.all_gather(head_in.astype(jnp.bfloat16), 'tp', axis=1, tiled=True)
        head_w = gather_weight(w_head, 0)
        logits = product('bc,ck->bk', head_full, head_w) + b_head
        class_local = logits.shape[1]
        class_ids = lax.axis_index('tp') * class_local + jnp.arange(class_local)
        is_label = class_ids[None, :] == labels[:, None]
        row_max = lax.pmax(jnp.max(logits, axis=1), 'tp')
        shifted = jnp.exp(logits - row_max[:, None])
        class_sums = lax.psum(jnp.stack([jnp.sum(shifted, axis=1),
                                         jnp.sum(jnp.where(is_label, logits, 0.0), axis=1)]), 'tp')
        log_norm = row_max + jnp.log(class_sums[0])
        loss = lax.psum(jnp.sum(log_norm - class_sums[1]), 'fsdp') / total_images

        d_logits = (shifted / class_sums[0][:, None] - is_label.astype(jnp.float32)) / total_images
        d_logits_bf = d_logits.astype(jnp.bfloat16)
        g_w_head = sum_to_piece(product('bc,bk->ck', head_full, d_logits_bf), 0)
        g_b_head = lax.psum(jnp.sum(d_logits, axis=0), 'fsdp')
        d_head_in = lax.psum_scatter(product('bk,ck->bc', d_logits_bf, head_w), 'tp', scatter_dimension=1, tiled=True)
        g_lnf_g = sum_to_piece(jnp.sum(d_head_in * head_std, axis=0), 0)
        g_lnf_b = sum_to_piece(jnp.sum(d_head_in, axis=0), 0)
        d_pooled = norm_backward(d_head_in, lnf_gain, head_std, head_inv, channels)
        d_resid = jnp.broadcast_to((d_pooled / tokens)[:, None, :], resid.shape)

        grad_lists = {name: [] for name in LAYER_NAMES}
        for layer in reversed(range(w_tok1.shape[0])):
            keep = saved[layer]
            grad_lists['b_ch2'].append(sum_to_piece(lead_sum(d_resid), 0))
            d_out_full = lax.all_gather(d_resid.astype(jnp.bfloat16), 'tp', axis=2, tiled=True)
            ch_w1 = gather_weight(w_ch1[layer], 0)
            ch_w2 = gather_weight(w_ch2[layer], 0)
            grad_lists['w_ch2'].append(sum_to_piece(product('bsd,bsc->dc', keep['ch_act'], d_out_full), 0))
            d_ch_pre = gelu_grad(keep['ch_pre'], product('bsc,dc->bsd', d_out_full, ch_w2))
            grad_lists['b_ch1'].append(sum_to_piece(lead_sum(d_ch_pre), 0))
            d_ch_pre_bf = d_ch_pre.astype(jnp.bfloat16)
            grad_lists['w_ch1'].append(sum_to_piece(product('bsc,bsd->cd', keep['full_in'], d_ch_pre_bf), 0))
            d_norm2 = lax.psum_scatter(product('bsd,cd->bsc', d_ch_pre_bf, ch_w1), 'tp', scatter_dimension=2, tiled=True)
            grad_lists['ln2_g'].append(sum_to_piece(lead_sum(d_norm2 * keep['norm2_std']), 0))
            grad_lists['ln2_b'].append(sum_to_piece(lead_sum(d_norm2), 0))
            d_mid = d_resid + norm_backward(d_norm2, ln2_gain[layer], keep['norm2_std'], keep['norm2_inv'], channels)
            d_mid_bf = d_mid.astype(jnp.bfloat16)
            tok_w1 = gather_weight(w_tok1[layer], 1)
            tok_w2 = gather_weight(w_tok2[layer], 0)
            grad_lists['w_tok2'].append(lax.psum(sum_to_piece(product('bcj,bsc->js', keep['tok_act'], d_mid_bf), 0), 'tp'))
            d_tok_pre = gelu_grad(keep['tok_pre'], product('bsc,js->bcj', d_mid_bf, tok_w2))
            grad_lists['b_tok1'].append(lax.psum(sum_to_piece(lead_sum(d_tok_pre), 0), 'tp'))
            d_tok_pre_bf = d_tok_pre.astype(jnp.bfloat16)
            grad_lists['w_tok1'].append(lax.psum(sum_to_piece(product('bsc,bcj->sj', keep['normed'], d_tok_pre_bf), 1), 'tp'))
            d_norm1 = product('bcj,sj->bsc', d_tok_pre_bf, tok_w1)
            grad_lists['ln1_g'].append(sum_to_piece(lead_sum(d_norm1 * keep['norm1_std']), 0))
            grad_lists['ln1_b'].append(sum_to_piece(lead_sum(d_norm1), 0))
            d_resid = d_mid + norm_backward(d_norm1, ln1_gain[layer], keep['norm1_std'], keep['norm1_inv'], channels)

        g_b_stem = sum_to_piece(lead_sum(d_resid), 0)
        g_w_stem = sum_to_piece(product('bsp,bsc->pc', patches, d_resid.astype(jnp.bfloat16)), 0)
        stacked = [jnp.stack(grad_lists[name][::-1]) for name in LAYER_NAMES]
        return tuple([loss, g_w_stem, g_b_stem] + stacked + [g_lnf_g, g_lnf_b, g_w_head, g_b_head])

    specs = weight_specs()
    return jax.shard_map(step, mesh=mesh, in_specs=(P('fsdp', None, None), P('fsdp')) + specs,
                         out_specs=(P(),) + specs, check_vma=False)
```

profile of v0, /device:TPU:1, one launch (start us, length us, event | category | flops | bytes accessed | tf_op | source)
XLA Modules:
  0.0 1846.9 jit_solution(13034297636698955492)
XLA Ops:
  8.0 55.1 %all_gather.83 = bf16[3072,128]{1,0:T(8,128)(2,1)S(1)} all-gather(bf16[48,128]{1,0:T(8,128)(2,1)S(1)} %convert_element_type.107), channel_id=1, replica_groups=mesh['tp'=4,'fsdp'=64] {'fsdp'}, dimensions={0}, use_global_device_ids=true | all-gather | bytes 798720 | tf_op jit(solution)/shard_map/all_gather | solution.py:16
  63.1 48.8 %all-gather.10 = f32[64,4,2]{1,2,0:T(2,128)S(1)} all-gather(f32[1,4,2]{1,2,0:T(2,128)} %bitcast.368), channel_id=1, replica_groups=mesh['tp'=4,'fsdp'=64] {'fsdp'}, dimensions={0}, use_global_device_ids=true | all-gather | bytes 2080 | tf_op jit(solution)/shard_map/all_gather | solution.py:20
  112.8 47.6 %all-gather = bf16[1,49,256]{1,0,2:T(2,128)(2,1)S(1)} all-gather(bf16[1,49,4]{1,0,2:T(2,128)(2,1)S(1)} %get-tuple-element.179), channel_id=3, replica_groups=mesh['tp'=4,'fsdp'=64] {'fsdp'}, dimensions={2}, use_global_device_ids=true | all-gather | bytes 25480 | tf_op jit(solution)/shard_map/all_gather | solution.py:16
  161.3 48.8 %all-gather.9 = f32[64,2,2]{2,1,0:T(2,128)S(1)} all-gather(f32[1,2,2]{2,1,0:T(2,128)S(1)} %bitcast.352), channel_id=1, replica_groups=mesh['tp'=4,'fsdp'=64] {'fsdp'}, dimensions={0}, use_global_device_ids=true | all-gather | bytes 1040 | tf_op jit(solution)/shard_map/all_gather | solution.py:20
  210.9 47.6 %all-gather.8 = f32[64,2,2]{2,1,0:T(2,128)S(1)} all-gather(f32[1,2,2]{2,1,0:T(2,128)S(1)} %bitcast.353), channel_id=1, replica_groups=mesh['tp'=4,'fsdp'=64] {'fsdp'}, dimensions={0}, use_global_device_ids=true | all-gather | bytes 1040 | tf_op jit(solution)/shard_map/all_gather | solution.py:20
  263.2 124.1 %all-reduce.31 = (f32[128]{0:T(128)}, f32[128]{0:T(128)S(1)}, f32[128]{0:T(128)S(1)}) all-reduce(f32[128]{0:T(128)S(1)} %dynamic-update-slice.2, f32[128]{0:T(128)S(1)} %dynamic-update-slice.1, f32[128]{0:T(128)S(1)} %dynamic-update-slice), channel_id=1, replica_groups=mesh['tp'=4,'fsdp'=64] {'fsdp'}, use_global_device_ids=true, to_apply=%add.2 | all-reduce | flops 384 | bytes 3072
  410.7 53.7 %all-gather.1 = bf16[1,256,49]{2,0,1:T(2,128)(2,1)S(1)} all-gather(bf16[1,4,49]{2,0,1:T(2,128)(2,1)S(1)} %get-tuple-element.175), channel_id=4, replica_groups=mesh['tp'=4,'fsdp'=64] {'fsdp'}, dimensions={1}, use_global_device_ids=true | all-gather | bytes 25480 | tf_op jit(solution)/shard_map/all_gather | solution.py:16
  474.6 49.9 %all-gather.12 = f32[64,2,2]{2,1,0:T(2,128)S(1)} all-gather(f32[1,2,2]{2,1,0:T(2,128)S(1)} %bitcast.354), channel_id=1, replica_groups=mesh['tp'=4,'fsdp'=64] {'fsdp'}, dimensions={0}, use_global_device_ids=true | all-gather | bytes 1040 | tf_op jit(solution)/shard_map/all_gather | solution.py:20
  524.7 46.9 %all-gather.11 = f32[64,2,2]{2,1,0:T(2,128)S(1)} all-gather(f32[1,2,2]{2,1,0:T(2,128)S(1)} %bitcast.355), channel_id=1, replica_groups=mesh['tp'=4,'fsdp'=64] {'fsdp'}, dimensions={0}, use_global_device_ids=true | all-gather | bytes 1040 | tf_op jit(solution)/shard_map/all_gather | solution.py:20
  586.0 52.6 %all-gather.13 = f32[64,8,2]{1,2,0:T(2,128)S(1)} all-gather(f32[1,8,2]{1,2,0:T(2,128)S(1)} %bitcast.369), channel_id=1, replica_groups=mesh['tp'=4,'fsdp'=64] {'fsdp'}, dimensions={0}, use_global_device_ids=true | all-gather | bytes 4160 | tf_op jit(solution)/shard_map/all_gather | solution.py:20
  638.7 47.4 %all-gather.3 = bf16[1,512,512]{2,1,0:T(8,128)(2,1)S(1)} all-gather(bf16[1,8,512]{2,1,0:T(8,128)(2,1)S(1)} %get-tuple-element.169), channel_id=6, replica_groups=mesh['tp'=4,'fsdp'=64] {'fsdp'}, dimensions={1}, use_global_device_ids=true | all-gather | bytes 532480 | tf_op jit(solution)/shard_map/all_gather | solution.py:16
  686.1 50.2 %all-gather.2 = bf16[1,512,512]{2,1,0:T(8,128)(2,1)S(1)} all-gather(bf16[1,8,512]{2,1,0:T(8,128)(2,1)S(1)} %get-tuple-element.171), channel_id=5, replica_groups=mesh['tp'=4,'fsdp'=64] {'fsdp'}, dimensions={1}, use_global_device_ids=true | all-gather | bytes 532480 | tf_op jit(solution)/shard_map/all_gather | solution.py:16
  748.1 46.9 %all-gather.14 = f32[64,2,2]{2,1,0:T(2,128)S(1)} all-gather(f32[1,2,2]{2,1,0:T(2,128)S(1)} %bitcast.356), channel_id=1, replica_groups=mesh['tp'=4,'fsdp'=64] {'fsdp'}, dimensions={0}, use_global_device_ids=true | all-gather | bytes 1040 | tf_op jit(solution)/shard_map/all_gather | solution.py:20
  795.1 49.4 %all-gather.4 = bf16[1,49,256]{1,0,2:T(2,128)(2,1)S(1)} all-gather(bf16[1,49,4]{1,0,2:T(2,128)(2,1)S(1)} %get-tuple-element.178), channel_id=7, replica_groups=mesh['tp'=4,'fsdp'=64] {'fsdp'}, dimensions={2}, use_global_device_ids=true | all-gather | bytes 25480 | tf_op jit(solution)/shard_map/all_gather | solution.py:16
  844.7 47.0 %all-gather.5 = bf16[1,256,49]{2,0,1:T(2,128)(2,1)S(1)} all-gather(bf16[1,4,49]{2,0,1:T(2,128)(2,1)S(1)} %get-tuple-element.174), channel_id=8, replica_groups=mesh['tp'=4,'fsdp'=64] {'fsdp'}, dimensions={1}, use_global_device_ids=true | all-gather | bytes 25480 | tf_op jit(solution)/shard_map/all_gather | solution.py:16
  931.6 56.7 %all-gather.6 = bf16[1,512,512]{2,1,0:T(8,128)(2,1)} all-gather(bf16[1,8,512]{2,1,0:T(8,128)(2,1)S(1)} %get-tuple-element.170), channel_id=9, replica_groups=mesh['tp'=4,'fsdp'=64] {'fsdp'}, dimensions={1}, use_global_device_ids=true | all-gather | bytes 532480 | tf_op jit(solution)/shard_map/all_gather | solution.py:16
  988.4 47.8 %all-gather.7 = bf16[1,512,512]{2,1,0:T(8,128)(2,1)} all-gather(bf16[1,8,512]{2,1,0:T(8,128)(2,1)S(1)} %get-tuple-element.168), channel_id=10, replica_groups=mesh['tp'=4,'fsdp'=64] {'fsdp'}, dimensions={1}, use_global_device_ids=true | all-gather | bytes 532480 | tf_op jit(solution)/shard_map/all_gather | solution.py:16
  1051.1 49.4 %all_gather.105 = bf16[512,250]{1,0:T(8,128)(2,1)S(1)} all-gather(bf16[8,250]{1,0:T(8,128)(2,1)S(1)} %convert_element_type.125), channel_id=1, replica_groups=mesh['tp'=4,'fsdp'=64] {'fsdp'}, dimensions={0}, use_global_device_ids=true | all-gather | bytes 260000 | tf_op jit(solution)/shard_map/all_gather | solution.py:16
  1100.6 14.6 reduce-scatter.9.cloned.1.call-done
  1154.2 29.5 %reduce-scatter.11.cloned.1.call-done = f32[64,128]{1,0:T(8,128)} async-done(((f32[64,512]{1,0:T(8,128)}), f32[64,128]{1,0:T(8,128)}) %reduce-scatter.11.cloned.1.call-update) | async-done | bytes 32784 | tf_op jit(solution)/shard_map/reduce_scatter | solution.py:119
  1217.7 73.8 %reduce-scatter.13.cloned.1.call-done = f32[64,49,128]{2,0,1:T(8,128)} async-done(((f32[64,49,512]{2,0,1:T(8,128)}), f32[64,49,128]{2,0,1:T(8,128)}) %reduce-scatter.13.cloned.1.call-update) | async-done | bytes 1605648 | tf_op jit(solution)/shard_map/reduce_scatter | solution.py:137
  1350.0 50.8 %all-gather.23.cloned.1.call-done = bf16[64,49,512]{2,0,1:T(8,128)(2,1)} async-done(((bf16[64,49,128]{2,0,1:T(8,128)(2,1)}), bf16[64,49,512]{2,0,1:T(8,128)(2,1)}) %all-gather.23.cloned.1.call-update) | async-done | bytes 3211280 | tf_op jit(solution)/shard_map/all_gather | solution.py:129
  1436.1 49.4 %reduce-scatter.15.cloned.1.call-done = f32[64,49,128]{2,0,1:T(8,128)} async-done(((f32[64,49,512]{2,0,1:T(8,128)}), f32[64,49,128]{2,0,1:T(8,128)}) %reduce-scatter.15.cloned.1.call-update) | async-done | bytes 1605648 | tf_op jit(solution)/shard_map/reduce_scatter | solution.py:137
  1561.4 256.9 %all-reduce.38 = (f32[]{:T(128)}, f32[128]{0:T(128)S(1)}, f32[128]{0:T(128)S(1)}, f32[128]{0:T(128)S(1)}, f32[128]{0:T(128)S(1)}, /*index=5*/f32[128]{0:T(128)S(...) all-reduce(f32[]{:T(128)} %fusion.125, ...), channel_id=1, replica_groups=mesh['tp'=4,'fsdp'=64] {'fsdp'}, use_global_device_ids=true, to_apply=%region_24.25 | all-reduce | flops 53627 | bytes 429016 | tf_op jit(solution)/shard_map/psum | solution.py:113
  (408 shorter events, 381.1 us)
Async XLA Ops:
  7.2 729.2 %all-gather.19.cloned.1.call-start = ((), (), s32[]{:S(2)}) async-start(), calls=%async_computation.5 | async-start | bytes 4014080 | tf_op jit(solution)/shard_map/all_gather | solution.py:91
  112.0 353.5 %copy-start.100 = (f32[1,256]{1,0:T(1,128)}, f32[1,256]{1,0:T(1,128)S(1)}, u32[]{:S(2)}) copy-start(f32[1,256]{1,0:T(1,128)S(1)} %get-tuple-element.177) | copy-start | bytes 3076
  112.0 796.6 %copy-start.102 = (f32[1,256]{1,0:T(1,128)}, f32[1,256]{1,0:T(1,128)S(1)}, u32[]{:S(2)}) copy-start(f32[1,256]{1,0:T(1,128)S(1)} %get-tuple-element.176) | copy-start | bytes 3076
  160.5 305.1 %copy-start.51 = (bf16[1,49,256]{2,1,0:T(8,128)(2,1)}, bf16[1,49,256]{2,1,0:T(8,128)(2,1)S(1)}, u32[]{:S(2)}) copy-start(bf16[1,49,256]{2,1,0:T(8,128)(2,1)S(1)} %copy.102) | copy-start | bytes 75268
  258.6 1259.7 %copy-start.63 = (f32[128]{0:T(128)}, f32[128]{0:T(128)S(1)}, u32[]{:S(2)}) copy-start(f32[128]{0:T(128)S(1)} %get-tuple-element.193) | copy-start | bytes 1540
  387.2 736.4 %copy-start.70 = (f32[128]{0:T(128)}, f32[128]{0:T(128)S(1)}, u32[]{:S(2)}) copy-start(f32[128]{0:T(128)S(1)} %get-tuple-element.126) | copy-start | bytes 1540
  396.7 76.8 %copy-start.5 = (f32[64,49,128]{2,0,1:T(8,128)}, f32[64,49,128]{2,0,1:T(8,128)S(1)}, u32[]{:S(2)}) copy-start(f32[64,49,128]{2,0,1:T(8,128)S(1)} %get-tuple-element.196) | copy-start | bytes 4816900
  474.5 417.4 %copy-start = (f32[64,49,128]{2,0,1:T(8,128)}, f32[64,49,128]{2,0,1:T(8,128)S(1)}, u32[]{:S(2)}) copy-start(f32[64,49,128]{2,0,1:T(8,128)S(1)} %get-tuple-element.150) | copy-start | bytes 4816900
  474.5 111.5 %copy-start.61 = (f32[2,8,512]{2,1,0:T(8,128)S(1)}, f32[2,8,512]{2,1,0:T(8,128)}, u32[]{:S(2)}) copy-start(f32[2,8,512]{2,1,0:T(8,128)} %param.32) | copy-start | bytes 98308
  474.5 111.5 %copy-start.62 = (f32[2,8,512]{2,1,0:T(8,128)S(1)}, f32[2,8,512]{2,1,0:T(8,128)}, u32[]{:S(2)}) copy-start(f32[2,8,512]{2,1,0:T(8,128)} %param.30) | copy-start | bytes 98308
  474.5 111.5 %copy-start.94 = (f32[2,8]{1,0:T(2,128)S(1)}, f32[2,8]{1,0:T(2,128)}, u32[]{:S(2)}) copy-start(f32[2,8]{1,0:T(2,128)} %param.31) | copy-start | bytes 196
  585.9 305.9 %reduce-scatter.7.cloned.1.call-start = ((), (), s32[]{:S(2)}) async-start(), calls=%async_computation.6 | async-start | bytes 8028160 | tf_op jit(solution)/shard_map/reduce_scatter | solution.py:95
  736.4 299.8 %copy-start.79 = (f32[1,512]{1,0:T(1,128)}, f32[1,512]{1,0:T(1,128)S(1)}, u32[]{:S(2)}) copy-start(f32[1,512]{1,0:T(1,128)S(1)} %get-tuple-element.172) | copy-start | bytes 6148
  747.4 288.8 %all-gather.21.cloned.1.call-start = ((), (), s32[]{:S(2)}) async-start(), calls=%async_computation.7 | async-start | bytes 4014080 | tf_op jit(solution)/shard_map/all_gather | solution.py:91
  931.6 183.5 %reduce-scatter.9.cloned.1.call-start = ((), (), s32[]{:S(2)}) async-start(), calls=%async_computation.8 | async-start | bytes 8028160 | tf_op jit(solution)/shard_map/reduce_scatter | solution.py:95
  1050.4 73.2 %copy-start.103 = (f32[128]{0:T(128)S(1)}, f32[128]{0:T(128)}, u32[]{:S(2)}) copy-start(f32[128]{0:T(128)} %get-tuple-element.125) | copy-start | bytes 1540
  1050.5 133.3 %reduce-scatter.11.cloned.1.call-start = ((), (), s32[]{:S(2)}) async-start(), calls=%async_computation.9 | async-start | bytes 163840 | tf_op jit(solution)/shard_map/reduce_scatter | solution.py:119
  1154.2 137.3 %reduce-scatter.13.cloned.1.call-start = ((), (), s32[]{:S(2)}) async-start(), calls=%async_computation.10 | async-start | bytes 8028160 | tf_op jit(solution)/shard_map/reduce_scatter | solution.py:137
  1217.6 73.9 %copy-start.33 = (f32[64,49]{0,1:T(8,128)S(1)}, f32[64,49]{0,1:T(8,128)}, u32[]{:S(2)}) copy-start(f32[64,49]{0,1:T(8,128)} %copy-done.32) | copy-start | bytes 37636
  1217.6 73.9 %copy-start.35 = (f32[64,49]{0,1:T(8,128)S(1)}, f32[64,49]{0,1:T(8,128)}, u32[]{:S(2)}) copy-start(f32[64,49]{0,1:T(8,128)} %copy-done.34) | copy-start | bytes 37636
  1217.6 93.1 %copy-start.58 = (bf16[1,256,49]{1,2,0:T(8,128)(2,1)S(1)}, bf16[1,256,49]{1,2,0:T(8,128)(2,1)}, u32[]{:S(2)}) copy-start(bf16[1,256,49]{1,2,0:T(8,128)(2,1)} %copy-done.57) | copy-start | bytes 75268
  1217.6 183.2 %all-gather.23.cloned.1.call-start = ((), (), s32[]{:S(2)}) async-start(), calls=%async_computation.11 | async-start | bytes 4014080 | tf_op jit(solution)/shard_map/all_gather | solution.py:129
  1350.0 135.5 %reduce-scatter.15.cloned.1.call-start = ((), (), s32[]{:S(2)}) async-start(), calls=%async_computation.12 | async-start | bytes 8028160 | tf_op jit(solution)/shard_map/reduce_scatter | solution.py:137
  1415.6 417.6 %all-reduce.37.cloned.1.call-start = ((), (), s32[]{:S(2)}) async-start(), calls=%async_computation.13 | async-start | bytes 12582912
  (92 other events, 935.8 us)
Sparse Core Ops, SparseCore 0:
  586.0 44.3 all-gather.18
  747.5 63.4 reduce-scatter.6
  931.7 47.9 all-gather.20
  1050.6 64.5 reduce-scatter.8
  1154.3 29.4 reduce-scatter.10
  1217.8 73.7 reduce-scatter.12
  1350.1 50.6 all-gather.22
  1415.7 69.7 reduce-scatter.14
  1550.3 207.6 all-reduce.36
where the time goes:
time: 1860 us; the launch traced here: 1850 us
  blocking collectives  1380 us (74%)
  waiting for transfers between devices  218 us (12%)
  matrix products  137 us (7%)
  other arithmetic  58.7 us (3%)
  local copies, waits for them, and re-layouts  29.9 us (2%)
  between operations  20.7 us (1%)
    all_gather x10, blocking collectives, gather_weight(): lax.all_gather(weight.astype(jnp.bfloat16), 'fsdp', axis=axis, tiled=True)  504 us
    all_gather x7, blocking collectives, gather_vector(): return lax.all_gather(values, 'fsdp', axis=values.ndim - 1, tiled=True)  342 us
    psum x1, blocking collectives, step(): loss = lax.psum(jnp.sum(log_norm - class_sums[1]), 'fsdp') / total_images  257 us
    dot_general x29, matrix products, product(): return jnp.einsum(form, left, right, preferred_element_type=jnp.float32)  137 us
    unnamed x1, blocking collectives  124 us
    reduce_scatter x2, waiting for transfers between devices, step(): lax.psum_scatter(product('bsd,cd->bsc', d_ch_pre_bf, ch_w1), 'tp', scatte...  123 us
    psum x5, blocking collectives, norm_backward(): moments = lax.psum(moments, 'tp') / width  57.9 us
    psum x5, blocking collectives, norm_forward(): moments = lax.psum(moments, 'tp') / width  57.3 us
  transfers between devices with their start and end apart: 9, of which 5 were waited for; matrix products, arithmetic and copies ran while one was open for 2% of the time, Pallas kernels for 0%

commit v1 on v0

v1 whole, which is shorter than its diff:
```python
import functools
import jax
import jax.numpy as jnp
from jax import lax
from jax.experimental import pallas as pl
from jax.experimental.pallas import tpu as pltpu
from jax.sharding import PartitionSpec as P

MESH = pl.DeviceIdType.MESH
SIZE = {'x': 4, 'y': 4, 'z': 8, 'c': 2}


class Net:
    def __init__(self, send_sems, recv_sems):
        self.send_sems, self.recv_sems, self.count, self.sent = send_sems, recv_sems, 0, []
        fsdp = lax.axis_index('fsdp')
        self.me = {'x': lax.axis_index('tp'), 'z': fsdp // 8, 'y': (fsdp // 2) % 4, 'c': fsdp % 2}

    def at(self, axis, offset):
        return lax.rem(self.me[axis] + (offset % SIZE[axis]), SIZE[axis])

    def device(self, axis, offset):
        pos = dict(self.me)
        pos[axis] = self.at(axis, offset)
        if axis == 'x':
            return {'tp': pos['x']}
        return {'fsdp': (pos['z'] * 4 + pos['y']) * 2 + pos['c']}

    def barrier(self):
        sem = pltpu.get_barrier_semaphore()
        total = 0
        for axis, size in SIZE.items():
            for offset in range(1, size):
                pl.semaphore_signal(sem, 1, device_id=self.device(axis, offset), device_id_type=MESH)
                total += 1
        pl.semaphore_wait(sem, total)

    def send(self, src, dst, axis, offset):
        i = self.count
        self.count += 1
        copy = pltpu.make_async_remote_copy(src_ref=src, dst_ref=dst, send_sem=self.send_sems.at[i], recv_sem=self.recv_sems.at[i],
                                            device_id=self.device(axis, offset), device_id_type=MESH)
        copy.start()
        self.sent.append(copy)
        return copy

    def finish(self):
        for copy in self.sent:
            copy.wait_send()


def region(tensor, **pos):
    ref, width = tensor
    rows = [pos.get(axis, slice(None)) for axis in 'zyc']
    if width is None:
        return ref.at[tuple([pos.get('x', slice(None))] + rows)]
    cols = slice(None)
    if 'x' in pos:
        cols = pl.ds(pl.multiple_of(pos['x'] * width, width), width)
    return ref.at[tuple(rows + [slice(None), cols])]


HALF = {'x': 'z', 'y': 'z', 'z': 'y'}


def half(axis, which):
    other = HALF[axis]
    n = SIZE[other] // 2
    return {other: pl.ds(which * n, n)}


class Gather:
    def __init__(self, net, tensors, first, middle, last):
        self.net, self.tensors, self.order = net, tensors, (first, middle, last)
        self.core = []

    def direct(self, axis, fixed):
        net, copies = self.net, []
        for t in self.tensors:
            blk = region(t, **{a: net.me[a] for a in fixed})
            for offset in range(1, SIZE[axis]):
                copies.append(net.send(blk, blk, axis, offset))
        return copies

    def phase1(self):
        self.recv = self.direct(self.order[0], 'zycx')

    def arrived(self):
        for copy in self.recv:
            copy.wait_recv()
        self.recv = []

    def phase2(self):
        self.recv = self.direct(self.order[1], [a for a in 'zycx' if a != self.order[0]])

    def to_core(self, **pos):
        net = self.net
        for t in self.tensors:
            blk = region(t, c=net.me['c'], **pos)
            self.core.append(net.send(blk, blk, 'c', 1))

    def ring(self, step):
        net, axis = self.net, self.order[2]
        n = SIZE[axis]
        for sign in (1, -1):
            pos = {axis: net.at(axis, -sign * (step - 1))}
            if step == n // 2:
                pos.update(half(axis, (1 - sign) // 2))
            for t in self.tensors:
                blk = region(t, c=net.me['c'], **pos)
                self.recv.append(net.send(blk, blk, axis, sign))

    def ring_arrived(self, step):
        net, axis = self.net, self.order[2]
        self.arrived()
        if step == 0:
            self.to_core(**{axis: net.me[axis]})
        elif step == SIZE[axis] // 2:
            self.to_core(**{axis: net.at(axis, step)})
        else:
            for sign in (1, -1):
                self.to_core(**{axis: net.at(axis, -sign * step)})

    def core_arrived(self):
        for copy in self.core:
            copy.wait_recv()


def gather_kernel(stem_p, head_p, ch1_p, ch2_p, small_p, stem_o, head_o, c10_o, c11_o, c20_o, c21_o, small_o, bias_o,
                  stem, head, c10, c11, c20, c21, slots, small, merged_bias, send_sems, recv_sems, local_sems, out_sems):
    net = Net(send_sems, recv_sems)
    me = net.me
    tens = {'stem': (stem, 128), 'head': (head, 256), 'c10': (c10, 512), 'c11': (c11, 512), 'c20': (c20, None), 'c21': (c21, None)}
    pieces = (('stem', stem_p), ('head', head_p), ('c10', ch1_p.at[0]), ('c11', ch1_p.at[1]), ('c20', ch2_p.at[0]), ('c21', ch2_p.at[1]))
    loads = [pltpu.make_async_copy(src, region(tens[name], **me), local_sems.at[i]) for i, (name, src) in enumerate(pieces)]
    loads.append(pltpu.make_async_copy(small_p, slots.at[me['x']], local_sems.at[len(pieces)]))
    for copy in loads:
        copy.start()
    net.barrier()
    for copy in loads:
        copy.wait()
    tiny = [net.send(slots.at[me['x']], slots.at[me['x']], 'x', offset) for offset in range(1, 4)]
    a = Gather(net, [tens['stem'], tens['head']], 'x', 'y', 'z')
    b = Gather(net, [tens['c10'], tens['c20']], 'y', 'z', 'x')
    c = Gather(net, [tens['c11'], tens['c21']], 'z', 'x', 'y')
    for g in (a, b, c):
        g.phase1()
    for copy in tiny:
        copy.wait_recv()
    merged = slots[0] + slots[1] + slots[2] + slots[3]
    small[me['z'], me['y'], me['c']] = merged[0:8]
    merged_bias[...] = merged[8:16]
    for g in (a, b, c):
        g.arrived()
        g.phase2()
    mine = small.at[me['z'], me['y'], me['c']]
    tiny = [net.send(mine, mine, 'y', offset) for offset in range(1, 4)]
    a.ring_arrived(0)
    a.ring(1)
    for copy in tiny:
        copy.wait_recv()
    mine = small.at[me['z'], :, me['c']]
    tiny = [net.send(mine, mine, 'z', offset) for offset in range(1, 8)]
    for g in (c, b):
        g.ring_arrived(0)
        g.ring(1)
    for copy in tiny:
        copy.wait_recv()
    mine = small.at[:, :, me['c']]
    tiny = [net.send(mine, mine, 'c', 1)]
    a.ring_arrived(1)
    a.ring(2)
    a.ring_arrived(2)
    a.ring(3)
    for g in (b, c):
        g.ring_arrived(1)
        g.ring(2)
    a.ring_arrived(3)
    a.ring(4)
    for g in (b, c, a):
        g.ring_arrived(SIZE[g.order[2]] // 2)
    outs = []

    def put(src, dst):
        copy = pltpu.make_async_copy(src, dst, out_sems.at[len(outs)])
        copy.start()
        outs.append(copy)

    for copy in tiny:
        copy.wait_recv()
    put(small, small_o)
    put(merged_bias, bias_o)
    b.core_arrived()
    put(c10, c10_o)
    put(c20, c20_o)
    c.core_arrived()
    put(c11, c11_o)
    put(c21, c21_o)
    a.core_arrived()
    put(stem, stem_o)
    put(head, head_o)
    net.finish()
    for copy in outs:
        copy.wait()


def gather_all(stem_p, head_p, ch1_p, ch2_p, small_p):
    bf = jnp.bfloat16
    shapes = [((8, 4, 2, 48, 512), bf), ((8, 4, 2, 8, 1024), bf), ((8, 4, 2, 8, 2048), bf), ((8, 4, 2, 8, 2048), bf),
              ((4, 8, 4, 2, 8, 512), bf), ((4, 8, 4, 2, 8, 512), bf)]
    outs = shapes + [((8, 4, 2, 8, 128), jnp.float32), ((8, 128), jnp.float32)]
    hbm = pl.BlockSpec(memory_space=pl.ANY)
    return pl.pallas_call(
        gather_kernel, out_shape=[jax.ShapeDtypeStruct(s, d) for s, d in outs], in_specs=[hbm] * 5, out_specs=[hbm] * 8,
        scratch_shapes=[pltpu.VMEM(s, d) for s, d in shapes] + [pltpu.VMEM((4, 16, 128), jnp.float32),
                        pltpu.VMEM((8, 4, 2, 8, 128), jnp.float32), pltpu.VMEM((8, 128), jnp.float32), pltpu.SemaphoreType.DMA((160,)), pltpu.SemaphoreType.DMA((160,)),
                        pltpu.SemaphoreType.DMA((7,)), pltpu.SemaphoreType.DMA((8,))],
        compiler_params=pltpu.CompilerParams(collective_id=0, has_side_effects=True, vmem_limit_bytes=48 << 20),
        name='gather_weights')(stem_p, head_p, ch1_p, ch2_p, small_p)


def part(tensor, ref, **pos):
    rows = [pos.get(axis, slice(None)) for axis in tensor['rows']]
    width = tensor['width']
    if width is None:
        return ref.at[tuple([pos.get('x', slice(None))] + rows)]
    cols = slice(None)
    if 'x' in pos:
        cols = pl.ds(pl.multiple_of(pos['x'] * width, width), width)
    return ref.at[tuple(rows + [slice(None), cols])]


def accumulate(dst, srcs):
    lead = dst.shape[:-2]
    total = 1
    for n in lead:
        total *= n

    def body(i, carry):
        idx = []
        for n in reversed(lead):
            idx.append(lax.rem(i, n))
            i = i // n
        idx = tuple(reversed(idx))
        value = dst[idx]
        for src in srcs:
            value = value + src[idx]
        dst[idx] = value
        return carry

    if total == 1:
        idx = (0,) * len(lead)
        value = dst[idx] if lead else dst[...]
        for src in srcs:
            value = value + (src[idx] if lead else src[...])
        if lead:
            dst[idx] = value
        else:
            dst[...] = value
    else:
        lax.fori_loop(0, total, body, 0)


class Reduce:
    def __init__(self, net, tensors, first, middle, last, load_sems):
        self.net, self.tensors, self.order, self.load_sems = net, tensors, (first, middle, last), load_sems
        self.loads, self.recv, self.ready = {}, {}, set()

    def targets(self):
        n = SIZE[self.order[0]]
        order = [n // 2]
        for d in range(n // 2 - 1, 0, -1):
            order += [d, n - d]
        return order + [0]

    def start(self, i):
        net, axis = self.net, self.order[0]
        off = self.targets()[i]
        self.loads[off] = []
        for k, t in enumerate(self.tensors):
            pos = {axis: net.at(axis, off)}
            full = dict(t, rows='zyc')
            src = part(full, t['grad'], c=net.me['c'], **pos)
            load = pltpu.make_async_copy(src, part(t, t['sum'], **pos), self.load_sems.at[i * len(self.tensors) + k])
            load.start()
            away = part(full, t['grad'], c=1 - net.me['c'], **pos)
            self.loads[off].append((load, net.send(away, part(t, t['peer'], **pos), 'c', 1)))

    def prepare(self, off):
        net, axis = self.net, self.order[0]
        off = off % SIZE[axis]
        if off in self.ready:
            return
        self.ready.add(off)
        for t, (load, peer) in zip(self.tensors, self.loads[off]):
            load.wait()
            peer.wait_recv()
            pos = {axis: net.at(axis, off)}
            accumulate(part(t, t['sum'], **pos), [part(t, t['peer'], **pos)])

    def ring(self, step):
        net, axis = self.net, self.order[0]
        n = SIZE[axis]
        off = n // 2 - step + 1
        for sign in (1, -1):
            self.prepare(sign * off)
        copies = []
        for which, sign in enumerate((1, -1)):
            pos = {axis: net.at(axis, sign * off)}
            cut = dict(pos, **half(axis, which))
            for k, t in enumerate(self.tensors):
                if step > 1:
                    self.recv[sign, k].wait_recv()
                    slot = t['ring'][which][step - 2]
                    accumulate(part(t, t['sum'], **(cut if step == 2 else pos)), [slot])
            if step <= n // 2:
                for k, t in enumerate(self.tensors):
                    src = part(t, t['sum'], **(cut if step == 1 else pos))
                    copies.append(((sign, k), net.send(src, t['ring'][which][step - 1], axis, sign)))
        self.recv = dict(copies)

    def direct(self, phase):
        net, axis = self.net, self.order[phase]
        fixed = {a: net.me[a] for a in self.order[:phase]}
        self.recv = []
        for t in self.tensors:
            for offset in range(1, SIZE[axis]):
                src = part(t, t['sum'], **fixed, **{axis: net.at(axis, offset)})
                self.recv.append(net.send(src, t['slots'][phase - 1].at[offset - 1], axis, offset))

    def direct_done(self, phase):
        net, axis = self.net, self.order[phase]
        fixed = {a: net.me[a] for a in self.order[:phase + 1]}
        for copy in self.recv:
            copy.wait_recv()
        for t in self.tensors:
            accumulate(part(t, t['sum'], **fixed), [t['slots'][phase - 1].at[i] for i in range(SIZE[axis] - 1)])


REDUCED = (('stem', 0, 48, 128), ('head', 0, 8, 256), ('c10', 1, 8, 512), ('c20', 1, 8, None), ('c11', 2, 8, 512), ('c21', 2, 8, None))
ORDERS = (('z', 'y', 'x'), ('x', 'z', 'y'), ('y', 'x', 'z'))


def block_shape(rows, width, axes):
    lead = tuple(SIZE[a] for a in 'zy' if a in axes)
    if width is None:
        return (((SIZE['x'],) if 'x' in axes else ()) + lead + (rows, 512))
    return lead + (rows, width * (SIZE['x'] if 'x' in axes else 1))


def reduce_shapes():
    shapes = []
    for name, colour, rows, width in REDUCED:
        first, middle, last = ORDERS[colour]
        whole = block_shape(rows, width, 'xzy')
        one = [whole, whole]
        rest = middle + last
        for which in (0, 1):
            for step in range(SIZE[first] // 2):
                shape = list(block_shape(rows, width, rest))
                if step == 0:
                    axis = HALF[first]
                    at = [a for a in ('x' if width is None else '') + 'zy' if a in rest].index(axis)
                    shape[at] //= 2
                one.append(tuple(shape))
        one.append((SIZE[middle] - 1,) + block_shape(rows, width, last))
        one.append((SIZE[last] - 1,) + block_shape(rows, width, ''))
        shapes.append(one)
    return shapes


def reduce_kernel(*refs):
    n = len(REDUCED)
    grads, (small_g, head_g) = refs[:n], refs[n:n + 2]
    pieces, (small_o, head_o) = refs[n + 2:2 * n + 2], refs[2 * n + 2:2 * n + 4]
    scratch = list(refs[2 * n + 4:])
    tensors = []
    for (name, colour, rows, width), grad, shapes in zip(REDUCED, grads, reduce_shapes()):
        bufs = [scratch.pop(0) for _ in shapes]
        steps = SIZE[ORDERS[colour][0]] // 2
        tensors.append(dict(rows='zy', width=width, grad=grad, sum=bufs[0], peer=bufs[1], colour=colour,
                            ring=(bufs[2:2 + steps], bufs[2 + steps:2 + 2 * steps]), slots=bufs[-2:]))
    small, small_peer, small_y, small_z, small_x, head, head_c, head_y, head_z, last, send_sems, recv_sems, load_sems, out_sems = scratch
    net = Net(send_sems, recv_sems)
    me = net.me
    net.barrier()
    c = me['c']
    red = [Reduce(net, [t for t in tensors if t['colour'] == k], *ORDERS[k], load_sems.at[k]) for k in range(3)]
    a, b, d = red
    loads = [pltpu.make_async_copy(small_g.at[:, :, c], small, out_sems.at[0]), pltpu.make_async_copy(head_g, head.at[0], out_sems.at[1])]
    for copy in loads:
        copy.start()
    tiny = [net.send(small_g.at[:, :, 1 - c], small_peer, 'c', 1), net.send(head_g, head_c, 'c', 1)]
    for i in range(4):
        for r in red:
            if i < len(r.targets()):
                r.start(i)
        if i > 0:
            a.start(3 + i)
    a.start(7)
    for r in red:
        r.ring(1)
    for copy in loads:
        copy.wait()
    for copy in tiny:
        copy.wait_recv()
    accumulate(small, [small_peer])
    head[0] = head[0] + head_c[...]
    a.ring(2)
    tiny = [net.send(small.at[:, net.at('y', i)], small_y.at[i - 1], 'y', i) for i in (1, 2, 3)]
    tiny += [net.send(head.at[0], head_y.at[i - 1], 'y', i) for i in (1, 2, 3)]
    b.ring(2)
    d.ring(2)
    a.ring(3)
    for copy in tiny:
        copy.wait_recv()
    accumulate(small.at[:, me['y']], [small_y.at[i] for i in range(3)])
    head[1] = head[0] + head_y[0] + head_y[1] + head_y[2]
    a.ring(4)
    tiny = [net.send(small.at[net.at('z', i), me['y']], small_z.at[i - 1], 'z', i) for i in range(1, 8)]
    tiny += [net.send(head.at[1], head_z.at[i - 1], 'z', i) for i in range(1, 8)]
    b.ring(3)
    b.direct(1)
    d.ring(3)
    d.direct(1)
    for copy in tiny:
        copy.wait_recv()
    mine = small[me['z'], me['y']]
    total = head[1]
    for i in range(7):
        mine = mine + small_z[i]
        total = total + head_z[i]
    small_x[3, 0:8] = mine
    small_x[3, 8:16] = total
    a.ring(5)
    a.direct(1)
    tiny = [net.send(small_x.at[3], small_x.at[i - 1], 'x', i) for i in (1, 2, 3)]
    d.direct_done(1)
    d.direct(2)
    a.direct_done(1)
    a.direct(2)
    b.direct_done(1)
    b.direct(2)
    for copy in tiny:
        copy.wait_recv()
    whole = small_x[0] + small_x[1] + small_x[2] + small_x[3]
    last[...] = whole
    outs = [pltpu.make_async_copy(last.at[0:8], small_o, out_sems.at[0]), pltpu.make_async_copy(last.at[8:16], head_o, out_sems.at[1])]
    for r in (d, a, b):
        r.direct_done(2)
    for i, (t, piece) in enumerate(zip(tensors, pieces)):
        outs.append(pltpu.make_async_copy(part(t, t['sum'], x=me['x'], y=me['y'], z=me['z']), piece, out_sems.at[2 + i]))
    for copy in outs:
        copy.start()
    net.finish()
    for copy in outs:
        copy.wait()


def reduce_all(grads, small, head):
    f32 = jnp.float32
    hbm = pl.BlockSpec(memory_space=pl.ANY)
    outs = [(rows, 512 if width is None else width) for _, _, rows, width in REDUCED] + [(8, 128), (8, 128)]
    bufs = [shape for one in reduce_shapes() for shape in one]
    bufs += [(8, 4, 8, 128), (8, 4, 8, 128), (3, 8, 8, 128), (7, 8, 128), (4, 16, 128), (2, 8, 128), (8, 128), (3, 8, 128), (7, 8, 128), (16, 128)]
    return pl.pallas_call(
        reduce_kernel, out_shape=[jax.ShapeDtypeStruct(s, f32) for s in outs], in_specs=[hbm] * 8, out_specs=[hbm] * 8,
        scratch_shapes=[pltpu.VMEM(s, f32) for s in bufs] + [pltpu.SemaphoreType.DMA((200,)), pltpu.SemaphoreType.DMA((200,)),
                        pltpu.SemaphoreType.DMA((3, 16)), pltpu.SemaphoreType.DMA((8,))],
        compiler_params=pltpu.CompilerParams(collective_id=1, has_side_effects=True, vmem_limit_bytes=62 << 20),
        name='reduce_gradients')(*grads, small, head)


EPS = 1e-6
BF = jnp.bfloat16
VECTORS = 13
PER_X = 42


def product(form, left, right):
    return jnp.einsum(form, left, right, preferred_element_type=jnp.float32)


def norm_forward(values, gain, shift):
    width = values.shape[-1]
    mean_val = jnp.sum(values, axis=-1, keepdims=True) / width
    square = jnp.sum(values * values, axis=-1, keepdims=True) / width
    inv_std = lax.rsqrt(jnp.maximum(square - mean_val * mean_val, 0.0) + EPS)
    standard = (values - mean_val) * inv_std
    return standard * gain + shift, standard, inv_std


def norm_backward(grad_out, gain, standard, inv_std):
    width = grad_out.shape[-1]
    grad_std = grad_out * gain
    first = jnp.sum(grad_std, axis=-1, keepdims=True) / width
    second = jnp.sum(grad_std * standard, axis=-1, keepdims=True) / width
    return inv_std * (grad_std - first - standard * second)


def gelu_grad(pre_act, grad_out):
    return jax.vjp(jax.nn.gelu, pre_act)[1](grad_out)[0]


def lead_sum(values):
    return jnp.sum(values.reshape(-1, values.shape[-1]), axis=0)


def pack_small(x, b_stem, ln1_g, ln1_b, ln2_g, ln2_b, b_ch2, lnf_g, lnf_b, b_ch1, w_tok1, w_tok2, b_tok1, b_head):
    vec = jnp.concatenate([b_stem[None], ln1_g, ln1_b, ln2_g, ln2_b, b_ch2, lnf_g[None], lnf_b[None]], axis=0).reshape(-1)
    vec = jnp.concatenate([vec, b_ch1.reshape(-1)])
    spread = lax.dynamic_update_slice(jnp.zeros((4 * PER_X,), jnp.float32), vec, (x * PER_X,))
    tok = jnp.concatenate([w_tok1.reshape(-1), w_tok2.reshape(-1), b_tok1.reshape(-1)])
    tok = jnp.where(x == 0, tok.astype(jnp.float32), 0.0)
    first = jnp.concatenate([spread, tok, jnp.zeros((1024 - 4 * PER_X - tok.shape[0],), jnp.float32)])
    head = lax.dynamic_update_slice(jnp.zeros((1024,), jnp.float32), b_head, (x * 256,))
    return jnp.concatenate([first, head]).reshape(16, 128)


def solution(mesh):
    def step(patches, labels, w_stem, b_stem, ln1_g, ln1_b, w_tok1, b_tok1, w_tok2,
             ln2_g, ln2_b, w_ch1, b_ch1, w_ch2, b_ch2, lnf_g, lnf_b, w_head, b_head):
        x = lax.axis_index('tp')
        images = patches.shape[0] // 4
        total = 4096.0
        small_p = pack_small(x, b_stem, ln1_g, ln1_b, ln2_g, ln2_b, b_ch2, lnf_g, lnf_b, b_ch1,
                             w_tok1.astype(BF), w_tok2.astype(BF), b_tok1, b_head)
        head_p = jnp.pad(w_head.astype(BF), ((0, 0), (0, 6)))
        stem, head, c10, c11, c20, c21, small, bias = gather_all(w_stem.astype(BF), head_p, w_ch1.astype(BF), w_ch2.astype(BF), small_p)
        stem, head = stem.reshape(3072, 512), head.reshape(512, 1024)
        ch1 = [c10.reshape(512, 2048), c11.reshape(512, 2048)]
        ch2 = [c20.reshape(2048, 512), c21.reshape(2048, 512)]
        small = small.reshape(64, 1024)
        vec = small[:, :4 * PER_X].reshape(64, 4, PER_X)
        chan = vec[:, :, :26].reshape(64, 4, VECTORS, 2).transpose(2, 1, 0, 3).reshape(VECTORS, 512)
        stem_b, lnf_gf, lnf_bf = chan[0], chan[11], chan[12]
        ln1_gf, ln1_bf, ln2_gf, ln2_bf, ch2_b = (chan[1 + 2 * i:3 + 2 * i] for i in range(5))
        ch1_b = vec[:, :, 26:].reshape(64, 4, 2, 8).transpose(2, 1, 0, 3).reshape(2, 2048)
        base = 4 * PER_X
        tok1 = small[:, base:base + 392].reshape(64, 2, 49, 4).transpose(1, 2, 0, 3).reshape(2, 49, 256).astype(BF)
        tok2 = small[:, base + 392:base + 784].reshape(64, 2, 4, 49).transpose(1, 0, 2, 3).reshape(2, 256, 49).astype(BF)
        tok_b = small[:, base + 784:base + 792].reshape(64, 2, 4).transpose(1, 0, 2).reshape(2, 256)
        head_b = bias.reshape(1024)

        mine = lax.dynamic_slice_in_dim(patches, x * images, images, 0)
        label = lax.dynamic_slice_in_dim(labels, x * images, images, 0)
        tokens = patches.shape[1]
        resid = product('bsp,pc->bsc', mine, stem) + stem_b
        saved = []
        for layer in range(2):
            n1, s1, i1 = norm_forward(resid, ln1_gf[layer], ln1_bf[layer])
            n1 = n1.astype(BF)
            tok_pre = product('bsc,sj->bcj', n1, tok1[layer]) + tok_b[layer]
            tok_act = jax.nn.gelu(tok_pre).astype(BF)
            resid = resid + product('bcj,js->bsc', tok_act, tok2[layer])
            n2, s2, i2 = norm_forward(resid, ln2_gf[layer], ln2_bf[layer])
            n2 = n2.astype(BF)
            ch_pre = product('bsc,cd->bsd', n2, ch1[layer]) + ch1_b[layer]
            ch_act = jax.nn.gelu(ch_pre).astype(BF)
            resid = resid + product('bsd,dc->bsc', ch_act, ch2[layer]) + ch2_b[layer]
            saved.append((n1, s1, i1, tok_pre, tok_act, n2, s2, i2, ch_pre, ch_act))
        pooled = jnp.mean(resid, axis=1)
        head_in, head_std, head_inv = norm_forward(pooled, lnf_gf, lnf_bf)
        head_in = head_in.astype(BF)
        column = jnp.arange(1024)
        valid = (column % 256) < 250
        class_id = jnp.where(valid, (column // 256) * 250 + column % 256, -1)
        logits = jnp.where(valid, product('bc,ck->bk', head_in, head) + head_b, -jnp.inf)
        is_label = class_id[None, :] == label[:, None]
        row_max = jnp.max(logits, axis=1)
        shifted = jnp.exp(logits - row_max[:, None])
        class_sum = jnp.sum(shifted, axis=1)
        picked = jnp.sum(jnp.where(is_label, logits, 0.0), axis=1)
        loss = jnp.sum(row_max + jnp.log(class_sum) - picked) / total
        d_logits = (shifted / class_sum[:, None] - is_label.astype(jnp.float32)) / total
        d_logits_bf = d_logits.astype(BF)
        g_head = product('bc,bk->ck', head_in, d_logits_bf)
        g_bias = jnp.where(column == 250, loss, jnp.sum(d_logits, axis=0))
        d_head = product('bk,ck->bc', d_logits_bf, head)
        g_lnf_g, g_lnf_b = jnp.sum(d_head * head_std, axis=0), jnp.sum(d_head, axis=0)
        d_pooled = norm_backward(d_head, lnf_gf, head_std, head_inv)
        d_resid = jnp.broadcast_to((d_pooled / tokens)[:, None, :], resid.shape)
        grad = {}
        for layer in (1, 0):
            n1, s1, i1, tok_pre, tok_act, n2, s2, i2, ch_pre, ch_act = saved[layer]
            grad['b_ch2', layer] = lead_sum(d_resid)
            d_bf = d_resid.astype(BF)
            grad['w_ch2', layer] = product('bsd,bsc->dc', ch_act, d_bf)
            d_pre = gelu_grad(ch_pre, product('bsc,dc->bsd', d_bf, ch2[layer]))
            grad['b_ch1', layer] = lead_sum(d_pre)
            d_pre = d_pre.astype(BF)
            grad['w_ch1', layer] = product('bsc,bsd->cd', n2, d_pre)
            d_n2 = product('bsd,cd->bsc', d_pre, ch1[layer])
            grad['ln2_g', layer], grad['ln2_b', layer] = lead_sum(d_n2 * s2), lead_sum(d_n2)
            d_mid = d_resid + norm_backward(d_n2, ln2_gf[layer], s2, i2)
            d_bf = d_mid.astype(BF)
            grad['w_tok2', layer] = product('bcj,bsc->js', tok_act, d_bf)
            d_tok = gelu_grad(tok_pre, product('bsc,js->bcj', d_bf, tok2[layer]))
            grad['b_tok1', layer] = lead_sum(d_tok)
            d_tok = d_tok.astype(BF)
            grad['w_tok1', layer] = product('bsc,bcj->sj', n1, d_tok)
            d_n1 = product('bcj,sj->bsc', d_tok, tok1[layer])
            grad['ln1_g', layer], grad['ln1_b', layer] = lead_sum(d_n1 * s1), lead_sum(d_n1)
            d_resid = d_mid + norm_backward(d_n1, ln1_gf[layer], s1, i1)
        g_b_stem = lead_sum(d_resid)
        g_stem = product('bsp,bsc->pc', mine, d_resid.astype(BF))

        def both(name):
            return [grad[name, 0], grad[name, 1]]

        chan = jnp.stack([g_b_stem] + both('ln1_g') + both('ln1_b') + both('ln2_g') + both('ln2_b') + both('b_ch2') + [g_lnf_g, g_lnf_b])
        vec = jnp.concatenate([chan.reshape(VECTORS, 4, 64, 2).transpose(2, 1, 0, 3).reshape(64, 4, 26),
                               jnp.stack(both('b_ch1')).reshape(2, 4, 64, 8).transpose(2, 1, 0, 3).reshape(64, 4, 16)], axis=2)
        tok = [jnp.stack(both('w_tok1')).reshape(2, 49, 64, 4).transpose(2, 0, 1, 3).reshape(64, 392),
               jnp.stack(both('w_tok2')).reshape(2, 64, 4, 49).transpose(1, 0, 2, 3).reshape(64, 392),
               jnp.stack(both('b_tok1')).reshape(2, 64, 4).transpose(1, 0, 2).reshape(64, 8)]
        small_g = jnp.concatenate([vec.reshape(64, 168)] + tok + [jnp.zeros((64, 64), jnp.float32)], axis=1)
        rows = (8, 4, 2, 8)
        grads = [g_stem.reshape(8, 4, 2, 48, 512), g_head.reshape(rows + (1024,)),
                 grad['w_ch1', 0].reshape(rows + (2048,)), grad['w_ch2', 0].reshape((4,) + rows + (512,)),
                 grad['w_ch1', 1].reshape(rows + (2048,)), grad['w_ch2', 1].reshape((4,) + rows + (512,))]
        o = reduce_all(grads, small_g.reshape(8, 4, 2, 8, 128), g_bias.reshape(8, 128))
        g_stem, g_head, c10, c20, c11, c21, small, bias = o
        small, bias = small.reshape(1024), bias.reshape(1024)
        vec = lax.dynamic_slice(small, (x * PER_X,), (PER_X,))
        chan = vec[:26].reshape(VECTORS, 2)
        pair = [chan[1 + 2 * i:3 + 2 * i] for i in range(5)]
        tok = small[base:]
        return (bias[250], g_stem, chan[0], pair[0], pair[1], tok[:392].reshape(2, 49, 4), tok[784:792].reshape(2, 4),
                tok[392:784].reshape(2, 4, 49), pair[2], pair[3], jnp.stack([c10, c11]), vec[26:].reshape(2, 8), jnp.stack([c20, c21]),
                pair[4], chan[11], chan[12], g_head[:, :250], lax.dynamic_slice(bias, (x * 256,), (250,)))

    vec_spec, layer_vec = P(('tp', 'fsdp')), P(None, ('tp', 'fsdp'))
    specs = (P('fsdp', 'tp'), vec_spec, layer_vec, layer_vec, P(None, None, 'fsdp'), P(None, 'fsdp'),
             P(None, 'fsdp', None), layer_vec, layer_vec, P(None, 'fsdp', 'tp'), layer_vec,
             P(None, ('tp', 'fsdp'), None), layer_vec, vec_spec, vec_spec, P('fsdp', 'tp'), P('tp'))
    return jax.shard_map(step, mesh=mesh, in_specs=(P('fsdp', None, None), P('fsdp')) + specs,
                         out_specs=(P(),) + specs, check_vma=False)
```

time: 1860 us -> 405 us (0.22)
  blocking collectives: 1380 us -> 0 us
  waiting for transfers between devices: 218 us -> 0 us
  Pallas kernels: 0 us -> 148 us
  other arithmetic: 58.7 us -> 27 us
  local copies, waits for them, and re-layouts: 29.9 us -> 57.9 us
  matrix products: 137 us -> 161 us
    all_gather x19 -> x0, blocking collectives: 865 us -> none  [the longest x10 504 us: gather_weight(): lax.all_gather(weight.astype(jnp.bfloat16), 'fsdp', axis=axis, tiled=True)]
    psum x13 -> x0, blocking collectives: 386 us -> none  [the longest x1 257 us: step(): loss = lax.psum(jnp.sum(log_norm - class_sums[1]), 'fsdp') / total_images]
    reduce_scatter x5 -> x0, waiting for transfers between devices: 167 us -> none  [the longest x2 123 us: step(): lax.psum_scatter(product('bsd,cd->bsc', d_ch_pre_bf, ch_w1), 'tp', scatte...]
    pallas_call x0 -> x2, Pallas kernels: none -> 148 us  [the longest x1 88.9 us: reduce_all(): pl.pallas_call(reduce_kernel, out_shape=[jax.ShapeDtypeStruct(s, f32) for...]
    unnamed x1 -> x0, blocking collectives: 124 us -> none
    all_gather x3 -> x0, waiting for transfers between devices: 50.8 us -> none  [the longest x1 50.8 us: step(): lax.all_gather(d_resid.astype(jnp.bfloat16), 'tp', axis=2, tiled=True)]
    dot_general x29, matrix products: 137 us -> 161 us  [product(): return jnp.einsum(form, left, right, preferred_element_type=jnp.float32)]
    reduce_sum x6 -> x5, other arithmetic: 23.9 us -> 5.08 us  [lead_sum(): return jnp.sum(values.reshape(-1, values.shape[-1]), axis=0)]
  transfers between devices with their start and end apart: 9 -> 0, of which waited for: 5 -> 0; matrix products, arithmetic and copies ran while one was open for 2% -> 0% of each run, Pallas kernels for 0% -> 0%
where the time goes in v1:
time: 405 us; the launch traced here: 397 us
  matrix products  161 us (40%)
  Pallas kernels  148 us (37%)
  local copies, waits for them, and re-layouts  57.9 us (14%)
  other arithmetic  27 us (7%)
    dot_general x29, matrix products, product(): return jnp.einsum(form, left, right, preferred_element_type=jnp.float32)  161 us
    pallas_call x1, Pallas kernels, reduce_all(): pl.pallas_call(reduce_kernel, out_shape=[jax.ShapeDtypeStruct(s, f32) for...  88.9 us
    pallas_call x1, Pallas kernels, gather_all(): pl.pallas_call(gather_kernel, out_shape=[jax.ShapeDtypeStruct(s, d) for s...  59.2 us
    convert_element_type x1, local copies, waits for them, and re-layouts, step(): ch_act = jax.nn.gelu(ch_pre).astype(BF)  11.1 us
    unnamed x227, local copies, waits for them, and re-layouts  9.9 us

profile of v1, /device:TPU:1, one launch (start us, length us, event | category | flops | bytes accessed | tf_op | source)
XLA Modules:
  0.0 397.1 jit_solution(4078416341191331392)
XLA Ops:
  10.4 59.2 %gather_weights.1 = (bf16[8,4,2,48,512]{4,3,2,1,0:T(8,128)(2,1)}, bf16[8,4,2,8,1024]{4,3,2,1,0:T(8,128)(2,1)S(1)}, bf16[8,4,2,8,2048]{4,3,2,1,0:T(8,128)(2,1)S(1...) custom-call(bf16[48,128]{1,0:T(8,128)(2,1)S(1)} %convert_element_typ, ...), custom_call_target="tpu_custom_call" | custom-call | tf_op jit(solution)/shard_map/gather_weights/pallas_call | solution.py:213
  77.2 4.6 %add_reduce_fusion.1 = (f32[16,49]{1,0:T(8,128)S(1)}, f32[16,49]{1,0:T(8,128)S(1)}, f32[16,49,512]{2,1,0:T(8,128)}) fusion(f32[512]{0:T(512)S(1)} %add.289, bf16[3072,512,1]{1,0,2:T(8,128)(2,1)S(1)} %bitcast.262, bf16[16,49,3072]{2,0,1:T(8,128)(2,1)S(1)} %constant_dynamic-slice_fusion), kind=kOutput, calls=%fused_computation.108 | convolution fusion | flops 2467854848 | bytes 9576576 | tf_op jit(solution)/shard_map/bsp,pc->bsc/dot_general | solution.py:481
  87.0 8.4 %multiply_convert_fusion.1 = (bf16[16,512,256]{2,1,0:T(8,128)(2,1)}, f32[16,512,256]{2,1,0:T(8,128)}) fusion(f32[256]{0:T(256)S(1)} %add.296, bf16[49,256,1]{0,1,2:T(8,128)(2,1)S(1)} %bitcast.237, f32[512]{0:T(512)} %add.293, f32[512]{0:T(512)} %mul.485, f32[16,49]{1,0:T(8,128)S(1)} %get-tuple-element.192, f32[16,49]{1,0:T(8,128)S(1)} %get-tuple-element.191, ...), kind=kOutput, calls=%fused_computation.24 | convolution fusion | flops 228900864 | bytes 14227072 | tf_op jit(solution)/shard_map/bsc,sj->bcj/dot_general | solution.py:481
  97.8 5.5 %fusion.110 = (f32[16,49]{1,0:T(8,128)S(1)}, f32[16,49]{1,0:T(8,128)S(1)}, f32[16,49,512]{2,1,0:T(8,128)}) fusion(bf16[256,49,1]{1,0,2:T(8,128)(2,1)S(1)} %bitcast.241, bf16[16,512,256]{2,1,0:T(8,128)(2,1)} %get-tuple-element.208, f32[16,49,512]{2,1,0:T(8,128)} %get-tuple-element.207, f32[512]{0:T(512)S(1)} %add.289), kind=kOutput, calls=%fused_computation.221 | convolution fusion | flops 207526368 | bytes 7438976 | tf_op jit(solution)/shard_map/bcj,js->bsc/dot_general | solution.py:481
  107.6 19.2 %multiply_convert_fusion.3 = (bf16[16,49,2048]{2,0,1:T(8,128)(2,1)}, f32[16,49,2048]{2,0,1:T(8,128)}) fusion(f32[2048]{0:T(1024)S(1)} %add.306, bf16[512,2048,1]{1,0,2:T(8,128)(2,1)S(1)} %bitcast.215, bf16[16,49,512]{2,1,0:T(8,128)(2,1)} %add_convert_fusion.2), kind=kOutput, calls=%fused_computation.46 | convolution fusion | flops 1660223488 | bytes 12541952 | tf_op jit(solution)/shard_map/bsc,cd->bsd/dot_general | solution.py:481
  127.1 6.8 %fusion.109 = (f32[16,49]{1,0:T(8,128)S(1)}, f32[16,49]{1,0:T(8,128)S(1)}, f32[16,49,512]{2,1,0:T(8,128)}) fusion(f32[512]{0:T(512)S(1)} %add.312, f32[16,49,512]{2,1,0:T(8,128)} %get-tuple-element.210, bf16[2048,512,1]{1,0,2:T(8,128)(2,1)} %bitcast.263, bf16[16,49,2048]{2,0,1:T(8,128)(2,1)} %get-tuple-element.211), kind=kOutput, calls=%fused_computation.220 | convolution fusion | flops 1646172672 | bytes 8528000 | tf_op jit(solution)/shard_map/bsd,dc->bsc/dot_general | solution.py:481
  134.9 7.1 %multiply_convert_fusion = (bf16[16,512,256]{2,1,0:T(8,128)(2,1)S(1)}, f32[16,512,256]{2,1,0:T(8,128)}) fusion(f32[256]{0:T(256)S(1)} %add.319, bf16[49,256,1]{0,1,2:T(8,128)(2,1)S(1)} %bitcast.239, f32[16,49,512]{2,1,0:T(8,128)} %get-tuple-element.213, f32[512]{0:T(512)S(1)} %add.316, f32[512]{0:T(512)S(1)} %mul.507, f32[16,49]{1,0:T(8,128)S(1)} %get-tuple-element.188, ...), kind=kOutput, calls=%fused_computation.23 | convolution fusion | flops 228499456 | bytes 14225024 | tf_op jit(solution)/shard_map/bsc,sj->bcj/dot_general | solution.py:481
  148.3 8.7 %multiply_convert_fusion.2 = (bf16[16,49,2048]{2,0,1:T(8,128)(2,1)}, f32[16,49,2048]{2,0,1:T(8,128)}) fusion(f32[2048]{0:T(1024)S(1)} %add.329, bf16[512,2048,1]{1,0,2:T(8,128)(2,1)} %bitcast.217, bf16[16,49,512]{2,1,0:T(8,128)(2,1)} %add_convert_fusion), kind=kOutput, calls=%fused_computation.45 | convolution fusion | flops 1660223488 | bytes 12541952 | tf_op jit(solution)/shard_map/bsc,cd->bsd/dot_general | solution.py:481
  157.3 5.4 %add_reduce_fusion = f32[16,512]{1,0:T(8,128)S(1)} fusion(f32[16,49,512]{2,1,0:T(8,128)} %get-tuple-element.216, bf16[2048,512,1]{1,0,2:T(8,128)(2,1)} %bitcast.265, bf16[16,49,2048]{2,0,1:T(8,128)(2,1)} %get-tuple-element.217, f32[512]{0:T(512)S(1)} %add.335), kind=kOutput, calls=%fused_computation.90 | convolution fusion | flops 1645363200 | bytes 6948864 | tf_op jit(solution)/shard_map/bsd,dc->bsc/dot_general | solution.py:481
  168.7 8.8 %fusion.115 = (f32[2048]{0:T(1024)S(1)}, bf16[16,49,2048]{2,0,1:T(8,128)(2,1)S(1)}) fusion(f32[16,49,2048]{2,0,1:T(8,128)} %get-tuple-element.218, f32[2048]{0:T(1024)S(1)} %copy-done.47, bf16[2048,512,1]{1,0,2:T(8,128)(2,1)} %bitcast.266, bf16[16,512]{1,0:T(8,128)(2,1)S(1)} %get-tuple-element.156), kind=kOutput, calls=%fused_computation.226 | convolution fusion | flops 1679489024 | bytes 11763712 | tf_op jit(solution)/shard_map/bsc,dc->bsd/dot_general | solution.py:481
  182.3 6.9 %fusion.126 = (f32[256]{0:T(256)S(1)}, bf16[16,512,256]{2,1,0:T(8,128)(2,1)S(1)}) fusion(f32[16,512,256]{2,1,0:T(8,128)S(1)} %bitcast.270, f32[256]{0:T(256)S(1)} %copy-done.90, bf16[256,49,1]{1,0,2:T(8,128)(2,1)S(1)} %bitcast.244, f32[16,49,512]{2,1,0:T(8,128)S(1)} %get-tuple-element.182), kind=kOutput, calls=%fused_computation.237 | convolution fusion | flops 252059392 | bytes 14215680 | tf_op jit(solution)/shard_map/bsc,js->bcj/dot_general | solution.py:481
  193.5 6.6 %fusion.114 = (f32[2048]{0:T(1024)S(1)}, bf16[16,49,2048]{2,0,1:T(8,128)(2,1)S(1)}) fusion(f32[16,49,2048]{2,0,1:T(8,128)S(1)} %bitcast.272, f32[2048]{0:T(1024)S(1)} %copy-done.74, bf16[2048,512,1]{1,0,2:T(8,128)(2,1)S(1)} %bitcast.264, bf16[16,49,512]{2,1,0:T(8,128)(2,1)S(1)} %convert_element_type.141), kind=kOutput, calls=%fused_computation.225 | convolution fusion | flops 1679489024 | bytes 12550144 | tf_op jit(solution)/shard_map/bsc,dc->bsd/dot_general | solution.py:481
  204.4 7.9 %fusion.127 = (f32[256]{0:T(256)S(1)}, bf16[16,512,256]{2,1,0:T(8,128)(2,1)}) fusion(f32[16,512,256]{2,1,0:T(8,128)S(1)} %bitcast.268, f32[256]{0:T(256)S(1)} %copy-done.88, bf16[256,49,1]{1,0,2:T(8,128)(2,1)S(1)} %bitcast.242, f32[16,49,512]{2,1,0:T(8,128)S(1)} %multiply_add_fusion.1), kind=kOutput, calls=%fused_computation.238 | convolution fusion | flops 252059392 | bytes 14215680 | tf_op jit(solution)/shard_map/bsc,js->bcj/dot_general | solution.py:481
  212.7 3.6 fusion.82
  218.3 4.9 %fusion.53 = f32[49,256,1]{0,1,2:T(8,128)S(1)} fusion(bf16[16,512,256]{2,1,0:T(8,128)(2,1)} %get-tuple-element.231, f32[512]{0:T(512)S(1)} %copy-done.82, f32[512]{0:T(512)S(1)} %copy-done.55, f32[16,49]{1,0:T(8,128)S(1)} %get-tuple-element.192, f32[16,49]{1,0:T(8,128)S(1)} %get-tuple-element.191, f32[16,49,512]{2,1,0:T(8,128)} %get-tuple-element.207, ...), kind=kOutput, calls=%fused_computation.64 | convolution fusion | flops 207929344 | bytes 5862528 | tf_op jit(solution)/shard_map/bsc,bcj->sj/dot_general | solution.py:481
  225.6 4.6 %fusion.61 = (f32[512]{0:T(512)S(1)}, f32[16,49]{1,0:T(8,128)S(1)}, f32[16,49]{1,0:T(8,128)S(1)}, f32[49,16,512]{2,0,1:T(8,128)S(1)}) fusion(f32[16,49]{1,0:T(8,128)S(1)} %get-tuple-element.192, f32[16,49]{1,0:T(8,128)S(1)} %get-tuple-element.191, f32[16,49,512]{2,1,0:T(8,128)} %get-tuple-element.207, f32[512]{0:T(512)S(1)} %copy-done.50, ...), kind=kOutput, calls=%fused_computation.74 | convolution fusion | flops 209131488 | bytes 7449344 | tf_op jit(solution)/shard_map/bcj,sj->bsc/dot_general | solution.py:481
  239.8 4.1 %fusion.33 = bf16[2048,16,49]{0,1,2:T(8,128)(2,1)S(1)} fusion(f32[16,49,2048]{2,0,1:T(8,128)} %get-tuple-element.218, f32[2048]{0:T(1024)S(1)} %copy-done.48), kind=kLoop, calls=%fused_computation.44 | loop fusion | flops 16056320 | bytes 9641984 | tf_op jit(solution)/shard_map/convert_element_type | solution.py:559
  244.0 11.1 %copy.277 = bf16[2048,16,49]{2,1,0:T(8,128)(2,1)} copy(bf16[2048,16,49]{0,1,2:T(8,128)(2,1)S(1)} %fusion.33) | data formatting | bytes 6422528 | tf_op jit(solution)/shard_map/convert_element_type | solution.py:559
  255.1 9.3 %fusion.50.refs_5_ = f32[4,8,4,2,8,512]{5,4,3,2,1,0:T(8,128)} fusion(bf16[4,8,4,2,8,16,49]{6,5,4,3,2,1,0:T(8,128)(2,1)} %bitcast.221, bf16[16,512]{1,0:T(8,128)(2,1)S(1)} %copy-done.59), kind=kOutput, calls=%fused_computation.63 | convolution fusion | flops 1644167168 | bytes 7421952 | tf_op jit(solution)/shard_map/bsd,bsc->dc/dot_general | solution.py:481
  264.4 6.0 %fusion.46 = f32[512,2048,1]{1,0,2:T(8,128)} fusion(bf16[16,49,512]{2,1,0:T(8,128)(2,1)S(1)} %copy-done.26, bf16[16,49,2048]{2,0,1:T(8,128)(2,1)S(1)} %copy-done.22), kind=kOutput, calls=%fused_computation.59 | convolution fusion | flops 1644167168 | bytes 8208384 | tf_op jit(solution)/shard_map/bsc,bsd->cd/dot_general | solution.py:481
  270.4 4.4 %fusion.75 = f32[2048,512,1]{1,0,2:T(8,128)} fusion(bf16[16,49,2048]{2,0,1:T(8,128)(2,1)S(1)} %copy-done.94, bf16[16,49,512]{2,1,0:T(8,128)(2,1)S(1)} %copy-done.28), kind=kOutput, calls=%fused_computation.117 | convolution fusion | flops 1644167168 | bytes 8208384 | tf_op jit(solution)/shard_map/bsd,bsc->dc/dot_general | solution.py:481
  274.9 6.4 %fusion.42 = f32[512,2048,1]{1,0,2:T(8,128)} fusion(bf16[16,49,512]{2,1,0:T(8,128)(2,1)S(1)} %copy-done.25, bf16[16,49,2048]{2,0,1:T(8,128)(2,1)S(1)} %copy-done.24), kind=kOutput, calls=%fused_computation.55 | convolution fusion | flops 1644167168 | bytes 8208384 | tf_op jit(solution)/shard_map/bsc,bsd->cd/dot_general | solution.py:481
  283.2 7.9 %fusion.34 = f32[3072,512,1]{1,0,2:T(8,128)} fusion(bf16[16,49,3072]{2,0,1:T(8,128)(2,1)S(1)} %bitcast.225, bf16[16,49,512]{2,1,0:T(8,128)(2,1)S(1)} %copy-done.29), kind=kOutput, calls=%fused_computation.47 | convolution fusion | flops 2466250752 | bytes 11911168 | tf_op jit(solution)/shard_map/bsp,bsc->pc/dot_general | solution.py:481
  291.1 88.9 %reduce_gradients.1 = (f32[48,128]{1,0:T(8,128)}, f32[8,256]{1,0:T(8,128)}, f32[8,512]{1,0:T(8,128)}, f32[8,512]{1,0:T(8,128)}, f32[8,512]{1,0:T(8,128)}, /*inde...) custom-call(f32[8,4,2,48,512]{4,3,2,1,0:T(8,128)} %bitcast.223, f32[8,4,2,8,1024]{4,3,2,1,0:T(8,128)} %bitcast.222, ...), custom_call_target="tpu_custom_call" | custom-call | tf_op jit(solution)/shard_map/reduce_gradients/pallas_call | solution.py:466
  (413 shorter events, 87.6 us)
Async XLA Ops:
  73.8 24.0 %copy-start.49 = (f32[512]{0:T(512)}, f32[512]{0:T(512)S(1)}, u32[]{:S(2)}) copy-start(f32[512]{0:T(512)S(1)} %add.289) | copy-start | bytes 6148
  77.2 9.0 %slice-start.2 = ((f32[64,1024]{0,1:T(8,128)}), f32[64,8]{0,1:T(8,128)S(1)}, s32[]{:S(2)}) async-start(f32[64,1024]{0,1:T(8,128)} %copy.232), calls=%async_computation.2 | async-start | bytes 8192 | tf_op jit(solution)/shard_map/slice | solution.py:542
  103.3 23.5 %copy-start.36 = (f32[16,49]{1,0:T(8,128)}, f32[16,49]{1,0:T(8,128)S(1)}, u32[]{:S(2)}) copy-start(f32[16,49]{1,0:T(8,128)S(1)} %get-tuple-element.189) | copy-start | bytes 9412
  103.3 23.5 %copy-start.38 = (f32[16,49]{1,0:T(8,128)}, f32[16,49]{1,0:T(8,128)S(1)}, u32[]{:S(2)}) copy-start(f32[16,49]{1,0:T(8,128)S(1)} %get-tuple-element.190) | copy-start | bytes 9412
  107.6 19.2 %copy-start.73 = (f32[2048]{0:T(1024)}, f32[2048]{0:T(1024)S(1)}, u32[]{:S(2)}) copy-start(f32[2048]{0:T(1024)S(1)} %add.306) | copy-start | bytes 24580
  107.6 19.2 %copy-start.67 = (f32[1,4,64,2]{2,1,3,0:T(4,128)S(1)}, f32[1,4,64,2]{2,1,3,0:T(4,128)}, u32[]{:S(2)}) copy-start(f32[1,4,64,2]{2,1,3,0:T(4,128)} %get-tuple-element.175) | copy-start | bytes 6148
  145.0 12.0 %copy-start.53 = (f32[512]{0:T(512)}, f32[512]{0:T(512)S(1)}, u32[]{:S(2)}) copy-start(f32[512]{0:T(512)S(1)} %mul.518) | copy-start | bytes 6148
  157.3 11.4 %copy-start.47 = (f32[2048]{0:T(1024)S(1)}, f32[2048]{0:T(1024)}, u32[]{:S(2)}) copy-start(f32[2048]{0:T(1024)} %copy-done.46) | copy-start | bytes 24580
  162.8 14.8 %copy-start.76 = (f32[16]{0:T(128)}, f32[16]{0:T(128)S(1)}, u32[]{:S(2)}) copy-start(f32[16]{0:T(128)S(1)} %get-tuple-element.205) | copy-start | bytes 196
  163.1 14.5 %copy-start.44 = (f32[512]{0:T(512)}, f32[512]{0:T(512)S(1)}, u32[]{:S(2)}) copy-start(f32[512]{0:T(512)S(1)} %mul.529) | copy-start | bytes 6148
  163.4 14.2 %copy-start.51 = (f32[512]{0:T(512)}, f32[512]{0:T(512)S(1)}, u32[]{:S(2)}) copy-start(f32[512]{0:T(512)S(1)} %add.340) | copy-start | bytes 6148
  163.8 13.8 %copy-start.69 = (f32[16]{0:T(128)}, f32[16]{0:T(128)S(1)}, u32[]{:S(2)}) copy-start(f32[16]{0:T(128)S(1)} %get-tuple-element.219) | copy-start | bytes 196
  164.1 13.5 %copy-start.40 = (s32[1024]{0:T(1024)}, s32[1024]{0:T(1024)S(1)}, u32[]{:S(2)}) copy-start(s32[1024]{0:T(1024)S(1)} %fusion.98) | copy-start | bytes 12292
  168.7 9.0 %copy-start.1 = (bf16[8,4,2,8,2048]{4,3,2,1,0:T(8,128)(2,1)S(1)}, bf16[8,4,2,8,2048]{4,3,2,1,0:T(8,128)(2,1)}, u32[]{:S(2)}) copy-start(bf16[8,4,2,8,2048]{4,3,2,1,0:T(8,128)(2,1)} %copy-done) | copy-start | bytes 6291460
  180.9 11.6 %slice-start.7 = ((s8[6422528]{0:T(1024)(128)(4,1)}), s8[4194304]{0:T(1024)(128)(4,1)S(1)}, s32[]{:S(2)}) async-start(s8[6422528]{0:T(1024)(128)(4,1)} %bitcast.271), calls=%async_computation.7 | async-start | bytes 8388608
  181.8 9.5 %copy-start.11 = (f32[16,49,512]{2,1,0:T(8,128)}, f32[16,49,512]{2,1,0:T(8,128)S(1)}, u32[]{:S(2)}) copy-start(f32[16,49,512]{2,1,0:T(8,128)S(1)} %get-tuple-element.182) | copy-start | bytes 4816900
  182.3 10.3 %slice-start.8 = ((s8[6422528]{0:T(1024)(128)(4,1)}), s8[2228224]{0:T(1024)(128)(4,1)S(1)}, s32[]{:S(2)}) async-start(s8[6422528]{0:T(1024)(128)(4,1)} %bitcast.271), calls=%async_computation.8 | async-start | bytes 4456448
  191.2 13.1 %slice-start.3 = ((s8[8388608]{0:T(1024)(128)(4,1)}), s8[4194304]{0:T(1024)(128)(4,1)S(1)}, s32[]{:S(2)}) async-start(s8[8388608]{0:T(1024)(128)(4,1)} %bitcast.267), calls=%async_computation.3 | async-start | bytes 8388608
  193.5 10.8 %slice-start.4 = ((s8[8388608]{0:T(1024)(128)(4,1)}), s8[4194304]{0:T(1024)(128)(4,1)S(1)}, s32[]{:S(2)}) async-start(s8[8388608]{0:T(1024)(128)(4,1)} %bitcast.267), calls=%async_computation.4 | async-start | bytes 8388608
  244.0 11.1 %copy-start.59 = (bf16[16,512]{1,0:T(8,128)(2,1)S(1)}, bf16[16,512]{1,0:T(8,128)(2,1)}, u32[]{:S(2)}) copy-start(bf16[16,512]{1,0:T(8,128)(2,1)} %copy-done.58) | copy-start | bytes 49156
  255.1 9.3 %copy-start.22 = (bf16[16,49,2048]{2,0,1:T(8,128)(2,1)S(1)}, bf16[16,49,2048]{2,0,1:T(8,128)(2,1)}, u32[]{:S(2)}) copy-start(bf16[16,49,2048]{2,0,1:T(8,128)(2,1)} %copy-done.21) | copy-start | bytes 9633796
  255.1 9.3 %copy-start.26 = (bf16[16,49,512]{2,1,0:T(8,128)(2,1)S(1)}, bf16[16,49,512]{2,1,0:T(8,128)(2,1)}, u32[]{:S(2)}) copy-start(bf16[16,49,512]{2,1,0:T(8,128)(2,1)} %add_convert_fusion) | copy-start | bytes 2408452
  264.4 18.8 %slice-start = ((s8[4816896]{0:T(1024)(128)(4,1)}), s8[4194304]{0:T(1024)(128)(4,1)S(1)}, s32[]{:S(2)}) async-start(s8[4816896]{0:T(1024)(128)(4,1)} %bitcast.224), calls=%async_computation | async-start | bytes 8388608
  270.4 12.8 %slice-start.1 = ((s8[4816896]{0:T(1024)(128)(4,1)}), s8[622592]{0:T(1024)(128)(4,1)S(1)}, s32[]{:S(2)}) async-start(s8[4816896]{0:T(1024)(128)(4,1)} %bitcast.224), calls=%async_computation.1 | async-start | bytes 1245184
  (80 other events, 415.4 us)
